TPU v7x, 32 devices: a whole 2x2x4 slice. The times are simulated.
32 devices in a mesh: dp: 4 (over y, core), tensor: 8 (over z, x).
Axes of the slice: x: 2, y: 2, z: 4, core: 2. Of those that a mesh axis runs over, the one named last changes fastest.
Arguments:
- query_latent: bfloat16 [64, 1536], P(('dp', 'tensor')), may hold values from -40 to 40
- key_value_latent: bfloat16 [64, 512], P(('dp', 'tensor')), may hold values from -40 to 40
- query_gain: float32 [1536], replicated, may hold values from 0.5 to 1.5
- key_value_gain: float32 [512], replicated, may hold values from 0.5 to 1.5
- q_up: bfloat16 [1536, 3072], P(None, 'tensor'), may hold values from -0.625 to 0.625
- kv_up: bfloat16 [512, 4096], P(None, 'tensor'), may hold values from -1 to 1
- grad_q: bfloat16 [64, 3072], P('dp', 'tensor'), may hold values from -0.23925781 to 0.23925781
- grad_kv: bfloat16 [64, 4096], P('dp', 'tensor'), may hold values from -0.23925781 to 0.23925781
Outputs:
- query_latent_gradient: float32 [64, 1536], P(('dp', 'tensor'))
- key_value_latent_gradient: float32 [64, 512], P(('dp', 'tensor'))
- d_q_up: float32 [1536, 3072], P('dp', 'tensor')
- d_kv_up: float32 [512, 4096], P('dp', 'tensor')
All inputs are finite; a program needn't handle non-finite values.
Results may differ from a plain program's by a relative error of at most 0.0029.
Values may be sent and summed in bfloat16 or wider, within the bound.
A program may use at most 64 MiB of HBM per device.

v0:
```python
import functools

import jax
import jax.numpy as jnp
from jax import lax
from jax.experimental import pallas as pl
from jax.experimental.pallas import tpu as pltpu
from jax.sharding import PartitionSpec as P

EPS = 1e-06
UNROLL = 64
LIMIT = 62 * 1024 * 1024


def repeat(count, step):
    if count <= UNROLL:
        for index in range(count):
            step(index)
    else:

        def body(index, carry):
            step(index)
            return carry

        lax.fori_loop(0, count, body, 0)


def unit_rows(raw):
    values = raw.astype(jnp.float32)
    inverse = lax.rsqrt(jnp.mean(values * values, axis=-1, keepdims=True) + EPS)
    return values * inverse, inverse


def backward_of_norm(incoming, unit, inverse, gain):
    scaled = gain * incoming
    return inverse * (scaled - unit * jnp.mean(scaled * unit, axis=-1, keepdims=True))


def wait_bytes(ref, sem):
    pltpu.make_async_copy(ref, ref, sem).wait()


def exchange(
    n_dp, n_t,
    lq_hbm, lkv_hbm, gain_q_hbm, gain_kv_hbm, q_up_hbm, kv_up_hbm, gq_hbm, gkv_hbm,
    g_recv, all_gq, all_gkv, normed_recv,
    lq, lkv, gain_q, gain_kv, q_up, kv_up, gq, gkv, normed_send, g_send,
    load_sem, send_sem, recv_sem, own_sem,
):
    me_d, me_t = lax.axis_index("dp"), lax.axis_index("tensor")
    me = me_d * n_t + me_t
    devices = n_dp * n_t
    rows = lq.shape[0]
    q_width, kv_width = lq.shape[1], lkv.shape[1]
    q_part, kv_part = q_width // n_dp, kv_width // n_dp

    barrier = pltpu.get_barrier_semaphore()

    def far(index):
        step = (index + 1) // 2
        return lax.rem(me_t + n_t // 2 + step * (2 * (index % 2) - 1) + n_t, n_t)

    def peer(offset):
        return lax.rem(me_d + offset % n_dp + 1, n_dp), far(offset // n_dp)

    def greet(index):
        pl.semaphore_signal(
            barrier, inc=1, device_id=peer(index), device_id_type=pl.DeviceIdType.MESH
        )

    repeat(devices - 1, greet)

    pairs = (
        (lq_hbm, lq),
        (lkv_hbm, lkv),
        (gain_q_hbm, gain_q),
        (gain_kv_hbm, gain_kv),
        (gq_hbm, gq),
        (gkv_hbm, gkv),
        (q_up_hbm, q_up),
        (kv_up_hbm, kv_up),
    )
    loads = [
        pltpu.make_async_copy(source, target, load_sem.at[index])
        for index, (source, target) in enumerate(pairs)
    ]
    for load in loads:
        load.start()

    for load in loads[:4]:
        load.wait()
    normed_q = gain_q[...] * unit_rows(lq[...])[0]
    normed_kv = gain_kv[...] * unit_rows(lkv[...])[0]
    for d in range(n_dp):
        piece = jnp.concatenate(
            (
                normed_q[:, d * q_part : (d + 1) * q_part],
                normed_kv[:, d * kv_part : (d + 1) * kv_part],
            ),
            axis=1,
        )
        normed_send[d] = piece.astype(jnp.bfloat16)

    own = [
        pltpu.make_async_copy(source, target, own_sem.at[index])
        for index, (source, target) in enumerate(
            (
                (g_send.at[me_t], g_recv.at[me_t]),
                (normed_send.at[me_d], normed_recv.at[me]),
                (gq, all_gq.at[me_d]),
                (gkv, all_gkv.at[me_d]),
            )
        )
    ]
    own[1].start()
    pl.semaphore_wait(barrier, devices - 1)

    def send(source, target, kind, device):
        pltpu.make_async_remote_copy(
            src_ref=source,
            dst_ref=target,
            send_sem=send_sem.at[kind],
            recv_sem=recv_sem.at[kind],
            device_id=device,
            device_id_type=pl.DeviceIdType.MESH,
        ).start()

    def send_sums(index):
        t = far(index)
        send(g_send.at[t], g_recv.at[me_t], 0, (me_d, t))

    def send_normed(index):
        d, t = peer(index)
        send(normed_send.at[d], normed_recv.at[me], 1, (d, t))

    def send_grads(index):
        d = lax.rem(me_d + index + 1, n_dp)
        send(gq, all_gq.at[me_d], 2, (d, me_t))
        send(gkv, all_gkv.at[me_d], 3, (d, me_t))

    repeat(devices - 1, send_normed)
    for load in loads[4:6]:
        load.wait()
    repeat(n_dp - 1, send_grads)
    own[2].start()
    own[3].start()

    for load in loads[6:]:
        load.wait()
    nt = (((1,), (1,)), ((), ()))
    g_q = lax.dot_general(gq[...], q_up[...], nt, preferred_element_type=jnp.float32)
    g_kv = lax.dot_general(gkv[...], kv_up[...], nt, preferred_element_type=jnp.float32)
    for t in range(n_t):
        g_send[t, :, :q_width] = g_q[t * rows : (t + 1) * rows].astype(g_send.dtype)
        g_send[t, :, q_width:] = g_kv[t * rows : (t + 1) * rows].astype(g_send.dtype)

    repeat(n_t - 1, send_sums)
    own[0].start()

    for copy in own:
        copy.wait()
    for sem in (send_sem, recv_sem):
        wait_bytes(g_recv.at[pl.ds(0, n_t - 1)], sem.at[0])
        wait_bytes(all_gq.at[pl.ds(0, n_dp - 1)], sem.at[2])
        wait_bytes(all_gkv.at[pl.ds(0, n_dp - 1)], sem.at[3])
        wait_bytes(normed_recv.at[pl.ds(0, devices - 1)], sem.at[1])


def finish(
    g_hbm, gq_hbm, gkv_hbm, normed_hbm, lq_hbm, lkv_hbm, gain_q_hbm, gain_kv_hbm,
    out_q_hbm, out_kv_hbm, d_q_hbm, d_kv_hbm,
    g, gq, gkv, normed_in, lq, lkv, gain_q, gain_kv, normed_all, out_q, out_kv, d_q, d_kv,
    load_sem, store_sem,
):
    pairs = (
        (normed_hbm, normed_in),
        (gq_hbm, gq),
        (gkv_hbm, gkv),
        (g_hbm, g),
        (lq_hbm, lq),
        (lkv_hbm, lkv),
        (gain_q_hbm, gain_q),
        (gain_kv_hbm, gain_kv),
    )
    loads = [
        pltpu.make_async_copy(source, target, load_sem.at[index])
        for index, (source, target) in enumerate(pairs)
    ]
    for load in loads:
        load.start()
    n_t, rows = g.shape[:2]
    devices = normed_in.shape[0]
    q_width = lq.shape[1]
    q_part = d_q.shape[0]
    group = max(1, 8 // rows)

    def gather_rows(index):
        block = jnp.concatenate(
            [normed_in[index * group + k].astype(jnp.float32) for k in range(group)], axis=0
        )
        start = index * group * rows
        if not isinstance(start, int):
            start = pl.multiple_of(start, group * rows)
        normed_all[pl.ds(start, group * rows), :] = block

    for load in loads:
        load.wait()
    total = g[0].astype(jnp.float32)
    for t in range(1, n_t):
        total += g[t].astype(jnp.float32)
    out_q[...] = backward_of_norm(total[:, :q_width], *unit_rows(lq[...]), gain_q[...])
    out_kv[...] = backward_of_norm(total[:, q_width:], *unit_rows(lkv[...]), gain_kv[...])
    repeat(devices // group, gather_rows)
    normed = normed_all[...].astype(jnp.bfloat16)
    tn = (((0,), (0,)), ((), ()))
    tokens = normed.shape[0]
    d_q[...] = lax.dot_general(
        normed[:, :q_part], gq[...].reshape(tokens, -1), tn, preferred_element_type=jnp.float32
    )
    stores = [
        pltpu.make_async_copy(source, target, store_sem.at[index])
        for index, (source, target) in enumerate(
            ((d_q, d_q_hbm), (d_kv, d_kv_hbm), (out_q, out_q_hbm), (out_kv, out_kv_hbm))
        )
    ]
    for index in (0, 2, 3):
        stores[index].start()
    d_kv[...] = lax.dot_general(
        normed[:, q_part:], gkv[...].reshape(tokens, -1), tn, preferred_element_type=jnp.float32
    )
    stores[1].start()
    for store in stores:
        store.wait()


def solution(mesh):
    n_dp, n_t = mesh.shape["dp"], mesh.shape["tensor"]

    def body(latent_q, latent_kv, gain_q, gain_kv, q_up, kv_up, grad_q, grad_kv):
        rows, q_width = latent_q.shape
        kv_width = latent_kv.shape[1]
        q_part, kv_part = q_width // n_dp, kv_width // n_dp
        part = q_part + kv_part
        width = q_width + kv_width
        devices = n_dp * n_t
        f32, bf16 = jnp.float32, jnp.bfloat16
        operands = (latent_q, latent_kv, gain_q, gain_kv, q_up, kv_up, grad_q, grad_kv)
        hbm = pl.BlockSpec(memory_space=pltpu.HBM)

        def like(x):
            return pltpu.VMEM(x.shape, x.dtype)

        moved = (
            jax.ShapeDtypeStruct((n_t, rows, width), bf16),
            jax.ShapeDtypeStruct((n_dp, *grad_q.shape), bf16),
            jax.ShapeDtypeStruct((n_dp, *grad_kv.shape), bf16),
            jax.ShapeDtypeStruct((devices, rows, part), bf16),
        )
        arrived = pl.pallas_call(
            functools.partial(exchange, n_dp, n_t),
            out_shape=moved,
            in_specs=[hbm] * len(operands),
            out_specs=(hbm,) * 4,
            scratch_shapes=[
                *(like(x) for x in operands),
                pltpu.VMEM((n_dp, rows, part), bf16),
                like(moved[0]),
                pltpu.SemaphoreType.DMA((8,)),
                pltpu.SemaphoreType.DMA((4,)),
                pltpu.SemaphoreType.DMA((4,)),
                pltpu.SemaphoreType.DMA((4,)),
            ],
            compiler_params=pltpu.CompilerParams(
                collective_id=0, has_side_effects=True, vmem_limit_bytes=LIMIT
            ),
        )(*operands)
        results = (
            jax.ShapeDtypeStruct((rows, q_width), f32),
            jax.ShapeDtypeStruct((rows, kv_width), f32),
            jax.ShapeDtypeStruct((q_part, grad_q.shape[1]), f32),
            jax.ShapeDtypeStruct((kv_part, grad_kv.shape[1]), f32),
        )
        sources = (*arrived, *operands[:4])
        return pl.pallas_call(
            finish,
            out_shape=results,
            in_specs=[hbm] * len(sources),
            out_specs=(hbm,) * 4,
            scratch_shapes=[
                *(like(x) for x in sources),
                pltpu.VMEM((devices * rows, part), f32),
                *(like(x) for x in results),
                pltpu.SemaphoreType.DMA((8,)),
                pltpu.SemaphoreType.DMA((4,)),
            ],
            compiler_params=pltpu.CompilerParams(vmem_limit_bytes=LIMIT),
        )(*sources)

    return jax.shard_map(
        body,
        mesh=mesh,
        in_specs=(
            P(("dp", "tensor"), None),
            P(("dp", "tensor"), None),
            P(),
            P(),
            P(None, "tensor"),
            P(None, "tensor"),
            P("dp", "tensor"),
            P("dp", "tensor"),
        ),
        out_specs=(
            P(("dp", "tensor"), None),
            P(("dp", "tensor"), None),
            P("dp", "tensor"),
            P("dp", "tensor"),
        ),
        check_vma=False,
    )
```

profile of v0, /device:TPU:0, one launch (start us, length us, event | category | flops | bytes accessed | tf_op | source)
XLA Modules:
  0.0 14.6 jit_solution(6916774716670226908)
XLA Ops:
  0.6 11.7 %shard_map.111 = (bf16[8,2,2048]{2,1,0:T(2,128)(2,1)}, bf16[4,16,384]{2,1,0:T(8,128)(2,1)}, bf16[4,16,512]{2,1,0:T(8,128)(2,1)}, bf16[32,2,512]{2,1,0:T(2,128)(2,1)}) custom-call(bf16[2,1536]{1,0:T(2,128)(2,1)} %lq_hbm.3, bf16[2,512]{1,0:T(2,128)(2,1)} %lkv_hbm.3, f32[1536]{0:T(1024)} %gain_q_hbm.3, f32[512]{0:T(512)} %gain_kv_hbm.3, ...), custom_call_target="tpu_custom_call" | custom-call | tf_op jit(solution)/shard_map/pallas_call | solution.py:259
  12.3 2.3 %shard_map.112 = (f32[2,1536]{1,0:T(2,128)}, f32[2,512]{1,0:T(2,128)}, f32[384,384]{1,0:T(8,128)}, f32[128,512]{1,0:T(8,128)}) custom-call(bf16[8,2,2048]{2,1,0:T(2,128)(2,1)} %get-tuple-element.8.g_hbm, bf16[4,16,384]{2,1,0:T(8,128)(2,1)} %get-tuple-element.9.gq_hbm, bf16[4,16,512]{2,1,0:T(8,128)(2,1)} %get-tuple-element.10.gkv_hbm, ...), custom_call_target="tpu_custom_call" | custom-call | tf_op jit(solution)/shard_map/pallas_call | solution.py:284
where the time goes:
time: 14.8 us; the launch traced here: 14.6 us
  Pallas kernels  14 us (95%)
  between operations  0.64 us (4%)
    pallas_call x1, Pallas kernels, body(): pl.pallas_call(functools.partial(exchange, n_dp, n_t), out_shape=moved, i...  11.7 us
    pallas_call x1, Pallas kernels, body(): pl.pallas_call(finish, out_shape=results, in_specs=[hbm] * len(sources),...  2.27 us

commit v1 on v0

--- a/solution.py
+++ b/solution.py
@@ -9,7 +9,7 @@
 
 EPS = 1e-06
 UNROLL = 64
-LIMIT = 62 * 1024 * 1024
+LIMIT = 24 * 1024 * 1024
 
 
 def repeat(count, step):
@@ -43,9 +43,9 @@
 def exchange(
     n_dp, n_t,
     lq_hbm, lkv_hbm, gain_q_hbm, gain_kv_hbm, q_up_hbm, kv_up_hbm, gq_hbm, gkv_hbm,
-    g_recv, all_gq, all_gkv, normed_recv,
-    lq, lkv, gain_q, gain_kv, q_up, kv_up, gq, gkv, normed_send, g_send,
-    load_sem, send_sem, recv_sem, own_sem,
+    g_recv, all_gq, all_gkv, normed_recv, lq, lkv, gain_q, gain_kv,
+    q_up, kv_up, normed_send, g_send,
+    load_sem, send_sem, recv_sem,
 ):
     me_d, me_t = lax.axis_index("dp"), lax.axis_index("tensor")
     me = me_d * n_t + me_t
@@ -54,6 +54,7 @@
     q_width, kv_width = lq.shape[1], lkv.shape[1]
     q_part, kv_part = q_width // n_dp, kv_width // n_dp
 
+    gq, gkv = all_gq.at[me_d], all_gkv.at[me_d]
     barrier = pltpu.get_barrier_semaphore()
 
     def far(index):
@@ -101,18 +102,7 @@
         )
         normed_send[d] = piece.astype(jnp.bfloat16)
 
-    own = [
-        pltpu.make_async_copy(source, target, own_sem.at[index])
-        for index, (source, target) in enumerate(
-            (
-                (g_send.at[me_t], g_recv.at[me_t]),
-                (normed_send.at[me_d], normed_recv.at[me]),
-                (gq, all_gq.at[me_d]),
-                (gkv, all_gkv.at[me_d]),
-            )
-        )
-    ]
-    own[1].start()
+    normed_recv[me] = normed_send[me_d]
     pl.semaphore_wait(barrier, devices - 1)
 
     def send(source, target, kind, device):
@@ -142,8 +132,6 @@
     for load in loads[4:6]:
         load.wait()
     repeat(n_dp - 1, send_grads)
-    own[2].start()
-    own[3].start()
 
     for load in loads[6:]:
         load.wait()
@@ -155,10 +143,7 @@
         g_send[t, :, q_width:] = g_kv[t * rows : (t + 1) * rows].astype(g_send.dtype)
 
     repeat(n_t - 1, send_sums)
-    own[0].start()
-
-    for copy in own:
-        copy.wait()
+    g_recv[me_t] = g_send[me_t]
     for sem in (send_sem, recv_sem):
         wait_bytes(g_recv.at[pl.ds(0, n_t - 1)], sem.at[0])
         wait_bytes(all_gq.at[pl.ds(0, n_dp - 1)], sem.at[2])
@@ -167,27 +152,17 @@
 
 
 def finish(
-    g_hbm, gq_hbm, gkv_hbm, normed_hbm, lq_hbm, lkv_hbm, gain_q_hbm, gain_kv_hbm,
+    g, gq, gkv, normed_in, lq, lkv, gain_q, gain_kv,
     out_q_hbm, out_kv_hbm, d_q_hbm, d_kv_hbm,
-    g, gq, gkv, normed_in, lq, lkv, gain_q, gain_kv, normed_all, out_q, out_kv, d_q, d_kv,
-    load_sem, store_sem,
+    normed_all, out_q, out_kv, d_q, d_kv,
+    store_sem,
 ):
-    pairs = (
-        (normed_hbm, normed_in),
-        (gq_hbm, gq),
-        (gkv_hbm, gkv),
-        (g_hbm, g),
-        (lq_hbm, lq),
-        (lkv_hbm, lkv),
-        (gain_q_hbm, gain_q),
-        (gain_kv_hbm, gain_kv),
-    )
-    loads = [
-        pltpu.make_async_copy(source, target, load_sem.at[index])
-        for index, (source, target) in enumerate(pairs)
+    stores = [
+        pltpu.make_async_copy(source, target, store_sem.at[index])
+        for index, (source, target) in enumerate(
+            ((d_q, d_q_hbm), (d_kv, d_kv_hbm), (out_q, out_q_hbm), (out_kv, out_kv_hbm))
+        )
     ]
-    for load in loads:
-        load.start()
     n_t, rows = g.shape[:2]
     devices = normed_in.shape[0]
     q_width = lq.shape[1]
@@ -203,13 +178,6 @@
             start = pl.multiple_of(start, group * rows)
         normed_all[pl.ds(start, group * rows), :] = block
 
-    for load in loads:
-        load.wait()
-    total = g[0].astype(jnp.float32)
-    for t in range(1, n_t):
-        total += g[t].astype(jnp.float32)
-    out_q[...] = backward_of_norm(total[:, :q_width], *unit_rows(lq[...]), gain_q[...])
-    out_kv[...] = backward_of_norm(total[:, q_width:], *unit_rows(lkv[...]), gain_kv[...])
     repeat(devices // group, gather_rows)
     normed = normed_all[...].astype(jnp.bfloat16)
     tn = (((0,), (0,)), ((), ()))
@@ -217,18 +185,18 @@
     d_q[...] = lax.dot_general(
         normed[:, :q_part], gq[...].reshape(tokens, -1), tn, preferred_element_type=jnp.float32
     )
-    stores = [
-        pltpu.make_async_copy(source, target, store_sem.at[index])
-        for index, (source, target) in enumerate(
-            ((d_q, d_q_hbm), (d_kv, d_kv_hbm), (out_q, out_q_hbm), (out_kv, out_kv_hbm))
-        )
-    ]
-    for index in (0, 2, 3):
-        stores[index].start()
+    stores[0].start()
     d_kv[...] = lax.dot_general(
         normed[:, q_part:], gkv[...].reshape(tokens, -1), tn, preferred_element_type=jnp.float32
     )
     stores[1].start()
+    total = g[0].astype(jnp.float32)
+    for t in range(1, n_t):
+        total += g[t].astype(jnp.float32)
+    out_q[...] = backward_of_norm(total[:, :q_width], *unit_rows(lq[...]), gain_q[...])
+    stores[2].start()
+    out_kv[...] = backward_of_norm(total[:, q_width:], *unit_rows(lkv[...]), gain_kv[...])
+    stores[3].start()
     for store in stores:
         store.wait()
 
@@ -245,28 +213,31 @@
         devices = n_dp * n_t
         f32, bf16 = jnp.float32, jnp.bfloat16
         operands = (latent_q, latent_kv, gain_q, gain_kv, q_up, kv_up, grad_q, grad_kv)
+        operands = [pltpu.with_memory_space_constraint(x, pltpu.HBM) for x in operands]
         hbm = pl.BlockSpec(memory_space=pltpu.HBM)
+
+        vmem = pl.BlockSpec(memory_space=pltpu.VMEM)
 
         def like(x):
             return pltpu.VMEM(x.shape, x.dtype)
 
         moved = (
-            jax.ShapeDtypeStruct((n_t, rows, width), bf16),
-            jax.ShapeDtypeStruct((n_dp, *grad_q.shape), bf16),
-            jax.ShapeDtypeStruct((n_dp, *grad_kv.shape), bf16),
-            jax.ShapeDtypeStruct((devices, rows, part), bf16),
+            pltpu.VMEM((n_t, rows, width), bf16),
+            pltpu.VMEM((n_dp, *grad_q.shape), bf16),
+            pltpu.VMEM((n_dp, *grad_kv.shape), bf16),
+            pltpu.VMEM((devices, rows, part), bf16),
+            *(like(x) for x in operands[:4]),
         )
         arrived = pl.pallas_call(
             functools.partial(exchange, n_dp, n_t),
             out_shape=moved,
             in_specs=[hbm] * len(operands),
-            out_specs=(hbm,) * 4,
+            out_specs=(vmem,) * len(moved),
             scratch_shapes=[
-                *(like(x) for x in operands),
+                *(like(x) for x in operands[4:6]),
                 pltpu.VMEM((n_dp, rows, part), bf16),
                 like(moved[0]),
                 pltpu.SemaphoreType.DMA((8,)),
-                pltpu.SemaphoreType.DMA((4,)),
                 pltpu.SemaphoreType.DMA((4,)),
                 pltpu.SemaphoreType.DMA((4,)),
             ],
@@ -280,21 +251,19 @@
             jax.ShapeDtypeStruct((q_part, grad_q.shape[1]), f32),
             jax.ShapeDtypeStruct((kv_part, grad_kv.shape[1]), f32),
         )
-        sources = (*arrived, *operands[:4])
+        arrived = [pltpu.with_memory_space_constraint(x, pltpu.VMEM) for x in arrived]
         return pl.pallas_call(
             finish,
             out_shape=results,
-            in_specs=[hbm] * len(sources),
+            in_specs=[vmem] * len(arrived),
             out_specs=(hbm,) * 4,
             scratch_shapes=[
-                *(like(x) for x in sources),
                 pltpu.VMEM((devices * rows, part), f32),
                 *(like(x) for x in results),
-                pltpu.SemaphoreType.DMA((8,)),
                 pltpu.SemaphoreType.DMA((4,)),
             ],
             compiler_params=pltpu.CompilerParams(vmem_limit_bytes=LIMIT),
-        )(*sources)
+        )(*arrived)
 
     return jax.shard_map(
         body,

time: 14.8 us -> 13.6 us (0.919)
  Pallas kernels: 14 us -> 12.8 us
    pallas_call x1, Pallas kernels: 2.27 us -> 1.25 us  [body(): pl.pallas_call(finish, out_shape=results, in_specs=[vmem] * len(arrived),...]
where the time goes in v1:
time: 13.6 us; the launch traced here: 13.4 us
  Pallas kernels  12.8 us (94%)
  between operations  0.64 us (5%)
    pallas_call x1, Pallas kernels, body(): pl.pallas_call(functools.partial(exchange, n_dp, n_t), out_shape=moved, i...  11.5 us
    pallas_call x1, Pallas kernels, body(): pl.pallas_call(finish, out_shape=results, in_specs=[vmem] * len(arrived),...  1.25 us

profile of v1, /device:TPU:0, one launch (start us, length us, event | category | flops | bytes accessed | tf_op | source)
XLA Modules:
  0.0 13.4 jit_solution(9772692861907722376)
XLA Ops:
  0.6 11.5 %shard_map.111 = (bf16[8,2,2048]{2,1,0:T(2,128)(2,1)S(1)}, bf16[4,16,384]{2,1,0:T(8,128)(2,1)S(1)}, bf16[4,16,512]{2,1,0:T(8,128)(2,1)S(1)}, bf16[32,2,512]{2,1,...) custom-call(bf16[2,1536]{1,0:T(2,128)(2,1)} %lq_hbm.1, ...), custom_call_target="tpu_custom_call" | custom-call | tf_op jit(solution)/shard_map/pallas_call | solution.py:231
  12.2 1.2 %shard_map.112 = (f32[2,1536]{1,0:T(2,128)}, f32[2,512]{1,0:T(2,128)}, f32[384,384]{1,0:T(8,128)}, f32[128,512]{1,0:T(8,128)}) custom-call(bf16[8,2,2048]{2,1,0:T(2,128)(2,1)S(1)} %get-tuple-element.12.g, bf16[4,16,384]{2,1,0:T(8,128)(2,1)S(1)} %get-tuple-element.13.gq, bf16[4,16,512]{2,1,0:T(8,128)(2,1)S(1)} %get-tuple-element.14.gkv, ...), custom_call_target="tpu_custom_call" | custom-call | tf_op jit(solution)/shard_map/pallas_call | solution.py:255

commit v2 on v1

--- a/solution.py
+++ b/solution.py
@@ -9,6 +9,7 @@
 
 EPS = 1e-06
 UNROLL = 64
+PIECES = 1
 LIMIT = 24 * 1024 * 1024
 
 
@@ -45,7 +46,7 @@
     lq_hbm, lkv_hbm, gain_q_hbm, gain_kv_hbm, q_up_hbm, kv_up_hbm, gq_hbm, gkv_hbm,
     g_recv, all_gq, all_gkv, normed_recv, lq, lkv, gain_q, gain_kv,
     q_up, kv_up, normed_send, g_send,
-    load_sem, send_sem, recv_sem,
+    load_sem, send_sem, recv_sem, permit_sem,
 ):
     me_d, me_t = lax.axis_index("dp"), lax.axis_index("tensor")
     me = me_d * n_t + me_t
@@ -53,40 +54,119 @@
     rows = lq.shape[0]
     q_width, kv_width = lq.shape[1], lkv.shape[1]
     q_part, kv_part = q_width // n_dp, kv_width // n_dp
-
     gq, gkv = all_gq.at[me_d], all_gkv.at[me_d]
-    barrier = pltpu.get_barrier_semaphore()
-
-    def far(index):
-        step = (index + 1) // 2
-        return lax.rem(me_t + n_t // 2 + step * (2 * (index % 2) - 1) + n_t, n_t)
-
-    def peer(offset):
-        return lax.rem(me_d + offset % n_dp + 1, n_dp), far(offset // n_dp)
-
-    def greet(index):
-        pl.semaphore_signal(
-            barrier, inc=1, device_id=peer(index), device_id_type=pl.DeviceIdType.MESH
-        )
-
-    repeat(devices - 1, greet)
-
-    pairs = (
-        (lq_hbm, lq),
-        (lkv_hbm, lkv),
-        (gain_q_hbm, gain_q),
-        (gain_kv_hbm, gain_kv),
-        (gq_hbm, gq),
-        (gkv_hbm, gkv),
-        (q_up_hbm, q_up),
-        (kv_up_hbm, kv_up),
-    )
-    loads = [
-        pltpu.make_async_copy(source, target, load_sem.at[index])
-        for index, (source, target) in enumerate(pairs)
-    ]
+    mesh = pl.DeviceIdType.MESH
+
+    def depth(d, t):
+        return t // 2 + t % 2 + d // 2
+
+    everyone = [(d, t) for d in range(n_dp) for t in range(n_t)]
+    everyone.sort(key=lambda place: depth(*place))
+    deepest = depth(*everyone[-1])
+
+    def remote(d, t):
+        return depth(d, t) >= max(1, deepest - 1)
+
+    def near(d, t):
+        return depth(d, t) < max(1, deepest - 1)
+
+    def first(d, t):
+        return (t == 0) & (d < 2)
+
+    def middle(d, t):
+        return near(d, t) & ((t != 0) | (d >= 2))
+
+    remotes = sum(int(remote(d, t)) for d, t in everyone)
+    nears = devices - remotes
+    am_near = near(me_d, me_t)
+    am_remote = remote(me_d, me_t)
+    am_last = depth(me_d, me_t) == deepest
+
+    def each(group, skip, act):
+        if devices <= UNROLL:
+            for d, t in everyone:
+                if not group(d, t):
+                    continue
+                if skip:
+                    pl.when((me_d != d) | (me_t != t))(functools.partial(act, d, t))
+                else:
+                    act(d, t)
+        else:
+
+            def step(index, carry):
+                d, t = lax.rem(index, n_dp), lax.div(index, n_dp)
+                wanted = group(d, t)
+                if skip:
+                    wanted &= index != me_t * n_dp + me_d
+                pl.when(wanted)(functools.partial(act, d, t))
+                return carry
+
+            lax.fori_loop(0, devices, step, 0)
+
+    def line(count, mine, wanted, act):
+        def step(index):
+            pl.when((mine != index) & wanted(index))(functools.partial(act, index))
+
+        repeat(count, step)
+
+    loads = []
+    for source, target, pieces in (
+        (lq_hbm, lq, 1),
+        (lkv_hbm, lkv, 1),
+        (gain_q_hbm, gain_q, 1),
+        (gain_kv_hbm, gain_kv, 1),
+        (gq_hbm, gq, 1),
+        (gkv_hbm, gkv, 1),
+        (kv_up_hbm, kv_up, 1),
+        (q_up_hbm, q_up, PIECES),
+    ):
+        size = source.shape[0] // pieces
+        for piece in range(pieces):
+            span = pl.ds(piece * size, size)
+            loads.append(
+                pltpu.make_async_copy(
+                    source.at[span], target.at[span], load_sem.at[len(loads)]
+                )
+            )
     for load in loads:
         load.start()
+
+    barrier = pltpu.get_barrier_semaphore()
+
+    def greet(d, t):
+        pl.semaphore_signal(barrier, inc=1, device_id=(d, t), device_id_type=mesh)
+
+    pl.when(am_near)(functools.partial(each, near, True, greet))
+    each(remote, True, greet)
+
+    def send(source, target, kind, d, t):
+        pltpu.make_async_remote_copy(
+            src_ref=source,
+            dst_ref=target,
+            send_sem=send_sem.at[kind],
+            recv_sem=recv_sem.at[kind],
+            device_id=(d, t),
+            device_id_type=mesh,
+        ).start()
+
+    def send_sums(d, t):
+        send(g_send.at[t], g_recv.at[me_t], 0, d, t)
+
+    def send_normed(d, t):
+        send(normed_send.at[d], normed_recv.at[me], 1, d, t)
+
+    def send_grads(d):
+        send(gq, all_gq.at[me_d], 2, d, me_t)
+        send(gkv, all_gkv.at[me_d], 3, d, me_t)
+
+    def permit(d, t):
+        pl.semaphore_signal(permit_sem, inc=1, device_id=(d, t), device_id_type=mesh)
+
+    def sums_to(group):
+        line(n_t, me_t, lambda t: group(me_d, t), lambda t: send_sums(me_d, t))
+
+    def grads_to(group):
+        line(n_dp, me_d, lambda d: group(d, me_t), send_grads)
 
     for load in loads[:4]:
         load.wait()
@@ -102,53 +182,66 @@
         )
         normed_send[d] = piece.astype(jnp.bfloat16)
 
+    @pl.when(am_last)
+    def _():
+        pl.semaphore_wait(barrier, devices - 1)
+        each(near, False, send_normed)
+        each(near, False, permit)
+
     normed_recv[me] = normed_send[me_d]
-    pl.semaphore_wait(barrier, devices - 1)
-
-    def send(source, target, kind, device):
-        pltpu.make_async_remote_copy(
-            src_ref=source,
-            dst_ref=target,
-            send_sem=send_sem.at[kind],
-            recv_sem=recv_sem.at[kind],
-            device_id=device,
-            device_id_type=pl.DeviceIdType.MESH,
-        ).start()
-
-    def send_sums(index):
-        t = far(index)
-        send(g_send.at[t], g_recv.at[me_t], 0, (me_d, t))
-
-    def send_normed(index):
-        d, t = peer(index)
-        send(normed_send.at[d], normed_recv.at[me], 1, (d, t))
-
-    def send_grads(index):
-        d = lax.rem(me_d + index + 1, n_dp)
-        send(gq, all_gq.at[me_d], 2, (d, me_t))
-        send(gkv, all_gkv.at[me_d], 3, (d, me_t))
-
-    repeat(devices - 1, send_normed)
-    for load in loads[4:6]:
+    nt = (((1,), (1,)), ((), ()))
+    for load in loads[4:7]:
         load.wait()
-    repeat(n_dp - 1, send_grads)
-
-    for load in loads[6:]:
-        load.wait()
-    nt = (((1,), (1,)), ((), ()))
-    g_q = lax.dot_general(gq[...], q_up[...], nt, preferred_element_type=jnp.float32)
     g_kv = lax.dot_general(gkv[...], kv_up[...], nt, preferred_element_type=jnp.float32)
     for t in range(n_t):
-        g_send[t, :, :q_width] = g_q[t * rows : (t + 1) * rows].astype(g_send.dtype)
         g_send[t, :, q_width:] = g_kv[t * rows : (t + 1) * rows].astype(g_send.dtype)
-
-    repeat(n_t - 1, send_sums)
+    size = q_width // PIECES
+    for piece in range(PIECES):
+        loads[7 + piece].wait()
+        span = slice(piece * size, (piece + 1) * size)
+        g_q = lax.dot_general(gq[...], q_up[span], nt, preferred_element_type=jnp.float32)
+        for t in range(n_t):
+            g_send[t, :, span] = g_q[t * rows : (t + 1) * rows].astype(g_send.dtype)
     g_recv[me_t] = g_send[me_t]
-    for sem in (send_sem, recv_sem):
-        wait_bytes(g_recv.at[pl.ds(0, n_t - 1)], sem.at[0])
+
+    @pl.when(am_near)
+    def _():
+        pl.semaphore_wait(barrier, nears - 1)
+        each(first, True, send_normed)
+        sums_to(first)
+        each(middle, True, send_normed)
+        sums_to(middle)
+        grads_to(near)
+        pl.semaphore_wait(permit_sem, remotes)
+        each(remote, False, send_normed)
+        sums_to(remote)
+        grads_to(remote)
+
+    @pl.when(am_remote)
+    def _():
+        @pl.when(jnp.logical_not(am_last))
+        def _():
+            pl.semaphore_wait(barrier, devices - 1)
+            each(first, False, send_normed)
+
+        sums_to(first)
+
+        @pl.when(jnp.logical_not(am_last))
+        def _():
+            each(middle, False, send_normed)
+            each(near, False, permit)
+
+        sums_to(middle)
+        each(remote, True, send_normed)
+        sums_to(remote)
+        grads_to(near)
+        grads_to(remote)
+
+    for sem in (recv_sem, send_sem):
         wait_bytes(all_gq.at[pl.ds(0, n_dp - 1)], sem.at[2])
         wait_bytes(all_gkv.at[pl.ds(0, n_dp - 1)], sem.at[3])
         wait_bytes(normed_recv.at[pl.ds(0, devices - 1)], sem.at[1])
+        wait_bytes(g_recv.at[pl.ds(0, n_t - 1)], sem.at[0])
 
 
 def finish(
@@ -237,9 +330,10 @@
                 *(like(x) for x in operands[4:6]),
                 pltpu.VMEM((n_dp, rows, part), bf16),
                 like(moved[0]),
-                pltpu.SemaphoreType.DMA((8,)),
+                pltpu.SemaphoreType.DMA((7 + PIECES,)),
                 pltpu.SemaphoreType.DMA((4,)),
                 pltpu.SemaphoreType.DMA((4,)),
+                pltpu.SemaphoreType.REGULAR,
             ],
             compiler_params=pltpu.CompilerParams(
                 collective_id=0, has_side_effects=True, vmem_limit_bytes=LIMIT

time: 13.6 us -> 12 us (0.88)
  Pallas kernels: 12.8 us -> 11.2 us
    pallas_call x1, Pallas kernels: 11.5 us -> 9.94 us  [body(): pl.pallas_call(functools.partial(exchange, n_dp, n_t), out_shape=moved, i...]
where the time goes in v2:
time: 12 us; the launch traced here: 11.8 us
  Pallas kernels  11.2 us (93%)
  between operations  0.64 us (5%)
    pallas_call x1, Pallas kernels, body(): pl.pallas_call(functools.partial(exchange, n_dp, n_t), out_shape=moved, i...  9.94 us
    pallas_call x1, Pallas kernels, body(): pl.pallas_call(finish, out_shape=results, in_specs=[vmem] * len(arrived),...  1.25 us

profile of v2, /device:TPU:0, one launch (start us, length us, event | category | flops | bytes accessed | tf_op | source)
XLA Modules:
  0.0 11.8 jit_solution(1537951339643435435)
XLA Ops:
  0.6 9.9 %shard_map.111 = (bf16[8,2,2048]{2,1,0:T(2,128)(2,1)S(1)}, bf16[4,16,384]{2,1,0:T(8,128)(2,1)S(1)}, bf16[4,16,512]{2,1,0:T(8,128)(2,1)S(1)}, bf16[32,2,512]{2,1,...) custom-call(bf16[2,1536]{1,0:T(2,128)(2,1)} %lq_hbm.1, ...), custom_call_target="tpu_custom_call" | custom-call | tf_op jit(solution)/shard_map/pallas_call | solution.py:324
  10.6 1.2 %shard_map.112 = (f32[2,1536]{1,0:T(2,128)}, f32[2,512]{1,0:T(2,128)}, f32[384,384]{1,0:T(8,128)}, f32[128,512]{1,0:T(8,128)}) custom-call(bf16[8,2,2048]{2,1,0:T(2,128)(2,1)S(1)} %get-tuple-element.12.g, bf16[4,16,384]{2,1,0:T(8,128)(2,1)S(1)} %get-tuple-element.13.gq, bf16[4,16,512]{2,1,0:T(8,128)(2,1)S(1)} %get-tuple-element.14.gkv, ...), custom_call_target="tpu_custom_call" | custom-call | tf_op jit(solution)/shard_map/pallas_call | solution.py:349

commit v3 on v1

v3 whole, which is shorter than its diff:
```python
import functools

import jax
import jax.numpy as jnp
from jax import lax
from jax.experimental import pallas as pl
from jax.experimental.pallas import tpu as pltpu
from jax.sharding import PartitionSpec as P

EPS = 1e-06
UNROLL = 64
LIMIT = 24 * 1024 * 1024


def repeat(count, step):
    if count <= UNROLL:
        for index in range(count):
            step(index)
    else:

        def body(index, carry):
            step(index)
            return carry

        lax.fori_loop(0, count, body, 0)


def unit_rows(raw):
    values = raw.astype(jnp.float32)
    inverse = lax.rsqrt(jnp.mean(values * values, axis=-1, keepdims=True) + EPS)
    return values * inverse, inverse


def backward_of_norm(incoming, unit, inverse, gain):
    scaled = gain * incoming
    return inverse * (scaled - unit * jnp.mean(scaled * unit, axis=-1, keepdims=True))


def weight_gradient(target, normed_all, all_grads, rows, columns):
    tokens = normed_all.shape[0]
    target[...] = lax.dot_general(
        normed_all[:, rows].astype(jnp.bfloat16),
        all_grads[:, :, columns].reshape(tokens, -1),
        (((0,), (0,)), ((), ())),
        preferred_element_type=jnp.float32,
    )


def wait_bytes(ref, sem):
    pltpu.make_async_copy(ref, ref, sem).wait()


def exchange(
    n_dp, n_t,
    lq_hbm, lkv_hbm, gain_q_hbm, gain_kv_hbm, q_up_hbm, kv_up_hbm, gq_hbm, gkv_hbm,
    g_recv, all_grads, normed_all, unit_q, unit_kv, inverse_q, inverse_kv, gain_q, gain_kv, d_q,
    lq, lkv, normed_recv, q_up, kv_up, normed_send, g_send,
    recv_sem,
):
    me_d, me_t = lax.axis_index("dp"), lax.axis_index("tensor")
    me = me_d * n_t + me_t
    devices = n_dp * n_t
    rows = lq.shape[0]
    q_width, kv_width = lq.shape[1], lkv.shape[1]
    q_part, kv_part = q_width // n_dp, kv_width // n_dp
    q_cols = q_up.shape[1]
    grads = all_grads.at[me_d]
    gq, gkv = grads.at[:, :q_cols], grads.at[:, q_cols:]
    mesh = pl.DeviceIdType.MESH

    def depth(d, t):
        return t // 2 + t % 2 + d // 2

    everyone = [(d, t) for d in range(n_dp) for t in range(n_t)]
    everyone.sort(key=lambda place: depth(*place))
    deepest = depth(*everyone[-1])

    def remote(d, t):
        return depth(d, t) >= max(1, deepest - 1)

    def near(d, t):
        return depth(d, t) < max(1, deepest - 1)

    def first(d, t):
        return (t == 0) & (d < 2)

    def middle(d, t):
        return near(d, t) & ((t != 0) | (d >= 2))

    remotes = sum(int(remote(d, t)) for d, t in everyone)
    nears = devices - remotes
    am_near = near(me_d, me_t)
    am_remote = remote(me_d, me_t)
    am_last = depth(me_d, me_t) == deepest

    def each(group, skip, act):
        if devices <= UNROLL:
            for d, t in everyone:
                if not group(d, t):
                    continue
                if skip:
                    pl.when((me_d != d) | (me_t != t))(functools.partial(act, d, t))
                else:
                    act(d, t)
        else:

            def step(index, carry):
                d, t = lax.rem(index, n_dp), lax.div(index, n_dp)
                wanted = group(d, t)
                if skip:
                    wanted &= index != me_t * n_dp + me_d
                pl.when(wanted)(functools.partial(act, d, t))
                return carry

            lax.fori_loop(0, devices, step, 0)

    def line(count, mine, wanted, act):
        def step(index):
            pl.when((mine != index) & wanted(index))(functools.partial(act, index))

        repeat(count, step)

    half = n_t // 2
    my_half = me_t // half
    group = max(1, 8 // rows)
    blocks = half // group

    def gather_rows(which, index):
        d, start = index // blocks, which * half + index % blocks * group
        source = d * n_t + start
        block = jnp.concatenate(
            [normed_recv[source + k].astype(jnp.float32) for k in range(group)], axis=0
        )
        start = source * rows
        if not isinstance(start, int):
            start = pl.multiple_of(start, group * rows)
        normed_all[pl.ds(start, group * rows), :] = block

    def talk(load_sem, send_sem, permit_sem):
        loads = [
            pltpu.make_async_copy(source, target, load_sem.at[index])
            for index, (source, target) in enumerate(
                (
                    (lq_hbm, lq),
                    (lkv_hbm, lkv),
                    (gain_q_hbm, gain_q),
                    (gain_kv_hbm, gain_kv),
                    (gkv_hbm, gkv),
                    (kv_up_hbm, kv_up),
                    (gq_hbm, gq),
                    (q_up_hbm, q_up),
                )
            )
        ]
        for load in loads:
            load.start()

        barrier = pltpu.get_barrier_semaphore()

        def greet(d, t):
            pl.semaphore_signal(barrier, inc=1, device_id=(d, t), device_id_type=mesh)

        pl.when(am_near)(functools.partial(each, near, True, greet))
        each(remote, True, greet)

        def send(source, target, kind, arrival, d, t):
            pltpu.make_async_remote_copy(
                src_ref=source,
                dst_ref=target,
                send_sem=send_sem.at[kind],
                recv_sem=recv_sem.at[arrival],
                device_id=(d, t),
                device_id_type=mesh,
            ).start()

        def send_sums(t):
            send(g_send.at[t], g_recv.at[me_t], 0, 0, me_d, t)

        def send_grads(d):
            send(grads, grads, 1, 1, d, me_t)

        def send_normed(d, t):
            send(normed_send.at[d], normed_recv.at[me], 2, 2 + my_half, d, t)

        def permit(d, t):
            pl.semaphore_signal(permit_sem, inc=1, device_id=(d, t), device_id_type=mesh)

        def sums_to(group):
            line(n_t, me_t, lambda t: group(me_d, t), send_sums)

        def grads_to(group):
            line(n_dp, me_d, lambda d: group(d, me_t), send_grads)

        for load in loads[:4]:
            load.wait()
        unit_q[...], inverse = unit_rows(lq[...])
        inverse_q[...] = jnp.broadcast_to(inverse, inverse_q.shape)
        unit_kv[...], inverse = unit_rows(lkv[...])
        inverse_kv[...] = jnp.broadcast_to(inverse, inverse_kv.shape)
        normed_q = gain_q[...] * unit_q[...]
        normed_kv = gain_kv[...] * unit_kv[...]
        for d in range(n_dp):
            piece = jnp.concatenate(
                (
                    normed_q[:, d * q_part : (d + 1) * q_part],
                    normed_kv[:, d * kv_part : (d + 1) * kv_part],
                ),
                axis=1,
            )
            normed_send[d] = piece.astype(jnp.bfloat16)

        @pl.when(am_last)
        def _():
            pl.semaphore_wait(barrier, devices - 1)
            each(first, False, send_normed)
            each(near, False, permit)
            each(middle, False, send_normed)

        normed_recv[me] = normed_send[me_d]
        nt = (((1,), (1,)), ((), ()))

        def partial_sums(needed, cotangent, weights, start):
            for load in needed:
                load.wait()
            sums = lax.dot_general(
                cotangent[...], weights[...], nt, preferred_element_type=jnp.float32
            )
            span = slice(start, start + sums.shape[1])
            for t in range(n_t):
                g_send[t, :, span] = sums[t * rows : (t + 1) * rows].astype(g_send.dtype)

        partial_sums(loads[4:6], gkv, kv_up, q_width)

        @pl.when(am_remote & jnp.logical_not(am_last))
        def _():
            pl.semaphore_wait(barrier, devices - 1)
            each(first, False, send_normed)
            each(near, False, permit)

        partial_sums(loads[6:], gq, q_up, 0)
        g_recv[me_t] = g_send[me_t]

        @pl.when(am_near)
        def _():
            pl.semaphore_wait(barrier, nears - 1)
            each(first, True, send_normed)
            sums_to(first)
            each(middle, True, send_normed)
            sums_to(middle)
            grads_to(near)
            pl.semaphore_wait(permit_sem, remotes)
            each(remote, False, send_normed)
            sums_to(remote)
            grads_to(remote)

        @pl.when(am_remote)
        def _():
            sums_to(first)

            @pl.when(jnp.logical_not(am_last))
            def _():
                each(middle, False, send_normed)

            sums_to(middle)
            each(remote, True, send_normed)
            sums_to(remote)
            grads_to(near)
            grads_to(remote)

        wait_bytes(g_recv.at[pl.ds(0, n_t - 1)], send_sem.at[0])
        wait_bytes(all_grads.at[pl.ds(0, n_dp - 1)], send_sem.at[1])
        wait_bytes(normed_recv.at[pl.ds(0, devices - 1)], send_sem.at[2])

    pl.run_scoped(
        talk,
        pltpu.SemaphoreType.DMA((8,)),
        pltpu.SemaphoreType.DMA((3,)),
        pltpu.SemaphoreType.REGULAR,
    )
    wait_bytes(all_grads.at[pl.ds(0, n_dp - 1)], recv_sem.at[1])
    for which in range(2):
        count = n_dp * half

        @pl.when(my_half == which)
        def _():
            wait_bytes(normed_recv.at[pl.ds(0, count - 1)], recv_sem.at[2 + which])

        @pl.when(my_half != which)
        def _():
            wait_bytes(normed_recv.at[pl.ds(0, count)], recv_sem.at[2 + which])

        repeat(n_dp * blocks, functools.partial(gather_rows, which))

    weight_gradient(d_q, normed_all, all_grads, slice(0, q_part), slice(0, q_cols))
    wait_bytes(g_recv.at[pl.ds(0, n_t - 1)], recv_sem.at[0])


def finish(
    g, all_grads, normed_all, unit_q, unit_kv, inverse_q, inverse_kv, gain_q, gain_kv, d_q,
    out_q_hbm, out_kv_hbm, d_q_hbm, d_kv_hbm,
    out_q, out_kv, d_kv,
    store_sem,
):
    stores = []

    def store(source, target):
        stores.append(pltpu.make_async_copy(source, target, store_sem.at[len(stores)]))
        stores[-1].start()

    store(d_q, d_q_hbm)
    n_t = g.shape[0]
    q_width = unit_q.shape[1]
    q_part, q_cols = d_q.shape
    weight_gradient(d_kv, normed_all, all_grads, slice(q_part, None), slice(q_cols, None))
    store(d_kv, d_kv_hbm)
    total = g[0].astype(jnp.float32)
    for t in range(1, n_t):
        total += g[t].astype(jnp.float32)
    out_q[...] = backward_of_norm(total[:, :q_width], unit_q[...], inverse_q[...], gain_q[...])
    out_kv[...] = backward_of_norm(total[:, q_width:], unit_kv[...], inverse_kv[...], gain_kv[...])
    store(out_q, out_q_hbm)
    store(out_kv, out_kv_hbm)
    for copy in stores:
        copy.wait()


def solution(mesh):
    n_dp, n_t = mesh.shape["dp"], mesh.shape["tensor"]

    def body(latent_q, latent_kv, gain_q, gain_kv, q_up, kv_up, grad_q, grad_kv):
        rows, q_width = latent_q.shape
        kv_width = latent_kv.shape[1]
        q_part, kv_part = q_width // n_dp, kv_width // n_dp
        part = q_part + kv_part
        width = q_width + kv_width
        devices = n_dp * n_t
        f32, bf16 = jnp.float32, jnp.bfloat16
        operands = (latent_q, latent_kv, gain_q, gain_kv, q_up, kv_up, grad_q, grad_kv)
        operands = [pltpu.with_memory_space_constraint(x, pltpu.HBM) for x in operands]
        hbm = pl.BlockSpec(memory_space=pltpu.HBM)

        vmem = pl.BlockSpec(memory_space=pltpu.VMEM)

        def like(x):
            return pltpu.VMEM(x.shape, x.dtype)

        results = (
            jax.ShapeDtypeStruct((rows, q_width), f32),
            jax.ShapeDtypeStruct((rows, kv_width), f32),
            jax.ShapeDtypeStruct((q_part, grad_q.shape[1]), f32),
            jax.ShapeDtypeStruct((kv_part, grad_kv.shape[1]), f32),
        )
        passed = (
            pltpu.VMEM((n_t, rows, width), bf16),
            pltpu.VMEM((n_dp, grad_q.shape[0], grad_q.shape[1] + grad_kv.shape[1]), bf16),
            pltpu.VMEM((devices * rows, part), f32),
            *(like(x) for x in results[:2] * 2),
            like(gain_q),
            like(gain_kv),
            like(results[2]),
        )
        arrived = pl.pallas_call(
            functools.partial(exchange, n_dp, n_t),
            out_shape=passed,
            in_specs=[hbm] * len(operands),
            out_specs=(vmem,) * len(passed),
            scratch_shapes=[
                like(latent_q),
                like(latent_kv),
                pltpu.VMEM((devices, rows, part), bf16),
                *(like(x) for x in operands[4:6]),
                pltpu.VMEM((n_dp, rows, part), bf16),
                like(passed[0]),
                pltpu.SemaphoreType.DMA((4,)),
            ],
            compiler_params=pltpu.CompilerParams(
                collective_id=0, has_side_effects=True, vmem_limit_bytes=LIMIT
            ),
        )(*operands)
        arrived = [pltpu.with_memory_space_constraint(x, pltpu.VMEM) for x in arrived]
        return pl.pallas_call(
            finish,
            out_shape=results,
            in_specs=[vmem] * len(arrived),
            out_specs=(hbm,) * 4,
            scratch_shapes=[
                *(like(x) for x in (*results[:2], results[3])),
                pltpu.SemaphoreType.DMA((4,)),
            ],
            compiler_params=pltpu.CompilerParams(vmem_limit_bytes=LIMIT),
        )(*arrived)

    return jax.shard_map(
        body,
        mesh=mesh,
        in_specs=(
            P(("dp", "tensor"), None),
            P(("dp", "tensor"), None),
            P(),
            P(),
            P(None, "tensor"),
            P(None, "tensor"),
            P("dp", "tensor"),
            P("dp", "tensor"),
        ),
        out_specs=(
            P(("dp", "tensor"), None),
            P(("dp", "tensor"), None),
            P("dp", "tensor"),
            P("dp", "tensor"),
        ),
        check_vma=False,
    )
```

time: 13.6 us -> 11.6 us (0.85)
  Pallas kernels: 12.8 us -> 10.7 us
    pallas_call x1, Pallas kernels: 11.5 us -> 9.78 us  [body(): pl.pallas_call(functools.partial(exchange, n_dp, n_t), out_shape=passed,...]
    pallas_call x1, Pallas kernels: 1.25 us -> 0.95 us  [body(): pl.pallas_call(finish, out_shape=results, in_specs=[vmem] * len(arrived),...]
where the time goes in v3:
time: 11.6 us; the launch traced here: 11.4 us
  Pallas kernels  10.7 us (92%)
  between operations  0.64 us (6%)
    pallas_call x1, Pallas kernels, body(): pl.pallas_call(functools.partial(exchange, n_dp, n_t), out_shape=passed,...  9.78 us
    pallas_call x1, Pallas kernels, body(): pl.pallas_call(finish, out_shape=results, in_specs=[vmem] * len(arrived),...  0.95 us

profile of v3, /device:TPU:0, one launch (start us, length us, event | category | flops | bytes accessed | tf_op | source)
XLA Modules:
  0.0 11.4 jit_solution(10102174842867052425)
XLA Ops:
  0.6 9.8 %shard_map.111 = (bf16[8,2,2048]{2,1,0:T(2,128)(2,1)S(1)}, bf16[4,16,896]{2,1,0:T(8,128)(2,1)S(1)}, f32[64,512]{1,0:T(8,128)S(1)}, f32[2,1536]{1,0:T(2,128)S(1)}...) custom-call(bf16[2,1536]{1,0:T(2,128)(2,1)} %lq_hbm.1, ...), custom_call_target="tpu_custom_call" | custom-call | tf_op jit(solution)/shard_map/pallas_call | solution.py:362
  10.4 1.0 %shard_map.112 = (f32[2,1536]{1,0:T(2,128)}, f32[2,512]{1,0:T(2,128)}, f32[384,384]{1,0:T(8,128)}, f32[128,512]{1,0:T(8,128)}) custom-call(bf16[8,2,2048]{2,1,0:T(2,128)(2,1)S(1)} %get-tuple-element.14.g, bf16[4,16,896]{2,1,0:T(8,128)(2,1)S(1)} %get-tuple-element.15.all_grads, f32[64,512]{1,0:T(8,128)S(1)} %get-tuple-element.16.normed_all, ...), custom_call_target="tpu_custom_call" | custom-call | tf_op jit(solution)/shard_map/pallas_call | solution.py:381

commit v4 on v3

--- a/solution.py
+++ b/solution.py
@@ -53,7 +53,7 @@
 def exchange(
     n_dp, n_t,
     lq_hbm, lkv_hbm, gain_q_hbm, gain_kv_hbm, q_up_hbm, kv_up_hbm, gq_hbm, gkv_hbm,
-    g_recv, all_grads, normed_all, unit_q, unit_kv, inverse_q, inverse_kv, gain_q, gain_kv, d_q,
+    g_recv, all_grads, normed_all, unit_q, unit_kv, inverse_q, inverse_kv, gain_q, gain_kv, d_q, d_kv,
     lq, lkv, normed_recv, q_up, kv_up, normed_send, g_send,
     recv_sem,
 ):
@@ -89,6 +89,7 @@
 
     remotes = sum(int(remote(d, t)) for d, t in everyone)
     nears = devices - remotes
+    am_first = first(me_d, me_t)
     am_near = near(me_d, me_t)
     am_remote = remote(me_d, me_t)
     am_last = depth(me_d, me_t) == deepest
@@ -191,6 +192,10 @@
         def grads_to(group):
             line(n_dp, me_d, lambda d: group(d, me_t), send_grads)
 
+        @pl.when(am_first)
+        def _():
+            pl.semaphore_wait(barrier, nears - 1)
+
         for load in loads[:4]:
             load.wait()
         unit_q[...], inverse = unit_rows(lq[...])
@@ -242,7 +247,7 @@
 
         @pl.when(am_near)
         def _():
-            pl.semaphore_wait(barrier, nears - 1)
+            pl.when(jnp.logical_not(am_first))(lambda: pl.semaphore_wait(barrier, nears - 1))
             each(first, True, send_normed)
             sums_to(first)
             each(middle, True, send_normed)
@@ -267,6 +272,22 @@
             grads_to(near)
             grads_to(remote)
 
+        wait_bytes(all_grads.at[pl.ds(0, n_dp - 1)], recv_sem.at[1])
+        for which in range(2):
+            count = n_dp * half
+
+            @pl.when(my_half == which)
+            def _():
+                wait_bytes(normed_recv.at[pl.ds(0, count - 1)], recv_sem.at[2 + which])
+
+            @pl.when(my_half != which)
+            def _():
+                wait_bytes(normed_recv.at[pl.ds(0, count)], recv_sem.at[2 + which])
+
+            repeat(n_dp * blocks, functools.partial(gather_rows, which))
+
+        weight_gradient(d_q, normed_all, all_grads, slice(0, q_part), slice(0, q_cols))
+        weight_gradient(d_kv, normed_all, all_grads, slice(q_part, None), slice(q_cols, None))
         wait_bytes(g_recv.at[pl.ds(0, n_t - 1)], send_sem.at[0])
         wait_bytes(all_grads.at[pl.ds(0, n_dp - 1)], send_sem.at[1])
         wait_bytes(normed_recv.at[pl.ds(0, devices - 1)], send_sem.at[2])
@@ -277,28 +298,13 @@
         pltpu.SemaphoreType.DMA((3,)),
         pltpu.SemaphoreType.REGULAR,
     )
-    wait_bytes(all_grads.at[pl.ds(0, n_dp - 1)], recv_sem.at[1])
-    for which in range(2):
-        count = n_dp * half
-
-        @pl.when(my_half == which)
-        def _():
-            wait_bytes(normed_recv.at[pl.ds(0, count - 1)], recv_sem.at[2 + which])
-
-        @pl.when(my_half != which)
-        def _():
-            wait_bytes(normed_recv.at[pl.ds(0, count)], recv_sem.at[2 + which])
-
-        repeat(n_dp * blocks, functools.partial(gather_rows, which))
-
-    weight_gradient(d_q, normed_all, all_grads, slice(0, q_part), slice(0, q_cols))
     wait_bytes(g_recv.at[pl.ds(0, n_t - 1)], recv_sem.at[0])
 
 
 def finish(
-    g, all_grads, normed_all, unit_q, unit_kv, inverse_q, inverse_kv, gain_q, gain_kv, d_q,
+    g, all_grads, normed_all, unit_q, unit_kv, inverse_q, inverse_kv, gain_q, gain_kv, d_q, d_kv,
     out_q_hbm, out_kv_hbm, d_q_hbm, d_kv_hbm,
-    out_q, out_kv, d_kv,
+    out_q, out_kv,
     store_sem,
 ):
     stores = []
@@ -310,8 +316,6 @@
     store(d_q, d_q_hbm)
     n_t = g.shape[0]
     q_width = unit_q.shape[1]
-    q_part, q_cols = d_q.shape
-    weight_gradient(d_kv, normed_all, all_grads, slice(q_part, None), slice(q_cols, None))
     store(d_kv, d_kv_hbm)
     total = g[0].astype(jnp.float32)
     for t in range(1, n_t):
@@ -358,6 +362,7 @@
             like(gain_q),
             like(gain_kv),
             like(results[2]),
+            like(results[3]),
         )
         arrived = pl.pallas_call(
             functools.partial(exchange, n_dp, n_t),
@@ -384,7 +389,7 @@
             in_specs=[vmem] * len(arrived),
             out_specs=(hbm,) * 4,
             scratch_shapes=[
-                *(like(x) for x in (*results[:2], results[3])),
+                *(like(x) for x in results[:2]),
                 pltpu.SemaphoreType.DMA((4,)),
             ],
             compiler_params=pltpu.CompilerParams(vmem_limit_bytes=LIMIT),

time: 11.6 us -> 11.5 us (level)
  no operation moved by 1% of the time
where the time goes in v4:
time: 11.5 us; the launch traced here: 11.4 us
  Pallas kernels  10.7 us (93%)
  between operations  0.64 us (6%)
    pallas_call x1, Pallas kernels, body(): pl.pallas_call(functools.partial(exchange, n_dp, n_t), out_shape=passed,...  9.78 us
    pallas_call x1, Pallas kernels, body(): pl.pallas_call(finish, out_shape=results, in_specs=[vmem] * len(arrived),...  0.94 us

profile of v4, /device:TPU:0, one launch (start us, length us, event | category | flops | bytes accessed | tf_op | source)
XLA Modules:
  0.0 11.4 jit_solution(12579074244538574449)
XLA Ops:
  0.6 9.8 %shard_map.111 = (bf16[8,2,2048]{2,1,0:T(2,128)(2,1)S(1)}, bf16[4,16,896]{2,1,0:T(8,128)(2,1)S(1)}, f32[64,512]{1,0:T(8,128)S(1)}, f32[2,1536]{1,0:T(2,128)S(1)}...) custom-call(bf16[2,1536]{1,0:T(2,128)(2,1)} %lq_hbm.1, ...), custom_call_target="tpu_custom_call" | custom-call | tf_op jit(solution)/shard_map/pallas_call | solution.py:367
  10.4 0.9 %shard_map.112 = (f32[2,1536]{1,0:T(2,128)}, f32[2,512]{1,0:T(2,128)}, f32[384,384]{1,0:T(8,128)}, f32[128,512]{1,0:T(8,128)}) custom-call(bf16[8,2,2048]{2,1,0:T(2,128)(2,1)S(1)} %get-tuple-element.15.g, bf16[4,16,896]{2,1,0:T(8,128)(2,1)S(1)} %get-tuple-element.16.all_grads, f32[64,512]{1,0:T(8,128)S(1)} %get-tuple-element.17.normed_all, ...), custom_call_target="tpu_custom_call" | custom-call | tf_op jit(solution)/shard_map/pallas_call | solution.py:386

commit v5 on v4

--- a/solution.py
+++ b/solution.py
@@ -55,106 +55,97 @@
     lq_hbm, lkv_hbm, gain_q_hbm, gain_kv_hbm, q_up_hbm, kv_up_hbm, gq_hbm, gkv_hbm,
     g_recv, all_grads, normed_all, unit_q, unit_kv, inverse_q, inverse_kv, gain_q, gain_kv, d_q, d_kv,
     lq, lkv, normed_recv, q_up, kv_up, normed_send, g_send,
-    recv_sem,
 ):
-    me_d, me_t = lax.axis_index("dp"), lax.axis_index("tensor")
-    me = me_d * n_t + me_t
-    devices = n_dp * n_t
-    rows = lq.shape[0]
-    q_width, kv_width = lq.shape[1], lkv.shape[1]
-    q_part, kv_part = q_width // n_dp, kv_width // n_dp
-    q_cols = q_up.shape[1]
-    grads = all_grads.at[me_d]
-    gq, gkv = grads.at[:, :q_cols], grads.at[:, q_cols:]
-    mesh = pl.DeviceIdType.MESH
-
-    def depth(d, t):
-        return t // 2 + t % 2 + d // 2
-
-    everyone = [(d, t) for d in range(n_dp) for t in range(n_t)]
-    everyone.sort(key=lambda place: depth(*place))
-    deepest = depth(*everyone[-1])
-
-    def remote(d, t):
-        return depth(d, t) >= max(1, deepest - 1)
-
-    def near(d, t):
-        return depth(d, t) < max(1, deepest - 1)
-
-    def first(d, t):
-        return (t == 0) & (d < 2)
-
-    def middle(d, t):
-        return near(d, t) & ((t != 0) | (d >= 2))
-
-    remotes = sum(int(remote(d, t)) for d, t in everyone)
-    nears = devices - remotes
-    am_first = first(me_d, me_t)
-    am_near = near(me_d, me_t)
-    am_remote = remote(me_d, me_t)
-    am_last = depth(me_d, me_t) == deepest
-
-    def each(group, skip, act):
-        if devices <= UNROLL:
-            for d, t in everyone:
-                if not group(d, t):
-                    continue
-                if skip:
-                    pl.when((me_d != d) | (me_t != t))(functools.partial(act, d, t))
-                else:
-                    act(d, t)
-        else:
-
-            def step(index, carry):
-                d, t = lax.rem(index, n_dp), lax.div(index, n_dp)
-                wanted = group(d, t)
-                if skip:
-                    wanted &= index != me_t * n_dp + me_d
-                pl.when(wanted)(functools.partial(act, d, t))
-                return carry
-
-            lax.fori_loop(0, devices, step, 0)
-
-    def line(count, mine, wanted, act):
-        def step(index):
-            pl.when((mine != index) & wanted(index))(functools.partial(act, index))
-
-        repeat(count, step)
-
-    half = n_t // 2
-    my_half = me_t // half
-    group = max(1, 8 // rows)
-    blocks = half // group
-
-    def gather_rows(which, index):
-        d, start = index // blocks, which * half + index % blocks * group
-        source = d * n_t + start
-        block = jnp.concatenate(
-            [normed_recv[source + k].astype(jnp.float32) for k in range(group)], axis=0
-        )
-        start = source * rows
-        if not isinstance(start, int):
-            start = pl.multiple_of(start, group * rows)
-        normed_all[pl.ds(start, group * rows), :] = block
-
-    def talk(load_sem, send_sem, permit_sem):
-        loads = [
-            pltpu.make_async_copy(source, target, load_sem.at[index])
-            for index, (source, target) in enumerate(
-                (
-                    (lq_hbm, lq),
-                    (lkv_hbm, lkv),
-                    (gain_q_hbm, gain_q),
-                    (gain_kv_hbm, gain_kv),
-                    (gkv_hbm, gkv),
-                    (kv_up_hbm, kv_up),
-                    (gq_hbm, gq),
-                    (q_up_hbm, q_up),
-                )
+    def talk(load_sem, send_sem, recv_sem, permit_sem):
+        loads = []
+
+        def fetch(*pairs):
+            for source, target in pairs:
+                loads.append(pltpu.make_async_copy(source, target, load_sem.at[len(loads)]))
+                loads[-1].start()
+
+        fetch((lq_hbm, lq), (lkv_hbm, lkv), (gain_q_hbm, gain_q), (gain_kv_hbm, gain_kv))
+        me_d, me_t = lax.axis_index("dp"), lax.axis_index("tensor")
+        me = me_d * n_t + me_t
+        devices = n_dp * n_t
+        rows = lq.shape[0]
+        q_width, kv_width = lq.shape[1], lkv.shape[1]
+        q_part, kv_part = q_width // n_dp, kv_width // n_dp
+        q_cols = q_up.shape[1]
+        grads = all_grads.at[me_d]
+        gq, gkv = grads.at[:, :q_cols], grads.at[:, q_cols:]
+        mesh = pl.DeviceIdType.MESH
+
+        def depth(d, t):
+            return t // 2 + t % 2 + d // 2
+
+        everyone = [(d, t) for d in range(n_dp) for t in range(n_t)]
+        everyone.sort(key=lambda place: depth(*place))
+        deepest = depth(*everyone[-1])
+
+        def remote(d, t):
+            return depth(d, t) >= max(1, deepest - 1)
+
+        def near(d, t):
+            return depth(d, t) < max(1, deepest - 1)
+
+        def first(d, t):
+            return (t == 0) & (d < 2)
+
+        def middle(d, t):
+            return near(d, t) & ((t != 0) | (d >= 2))
+
+        remotes = sum(int(remote(d, t)) for d, t in everyone)
+        nears = devices - remotes
+        am_first = first(me_d, me_t)
+        am_near = near(me_d, me_t)
+        am_remote = remote(me_d, me_t)
+        am_last = depth(me_d, me_t) == deepest
+
+        def each(group, skip, act):
+            if devices <= UNROLL:
+                for d, t in everyone:
+                    if not group(d, t):
+                        continue
+                    if skip:
+                        pl.when((me_d != d) | (me_t != t))(functools.partial(act, d, t))
+                    else:
+                        act(d, t)
+            else:
+
+                def step(index, carry):
+                    d, t = lax.rem(index, n_dp), lax.div(index, n_dp)
+                    wanted = group(d, t)
+                    if skip:
+                        wanted &= index != me_t * n_dp + me_d
+                    pl.when(wanted)(functools.partial(act, d, t))
+                    return carry
+
+                lax.fori_loop(0, devices, step, 0)
+
+        def line(count, mine, wanted, act):
+            def step(index):
+                pl.when((mine != index) & wanted(index))(functools.partial(act, index))
+
+            repeat(count, step)
+
+        half = n_t // 2
+        my_half = me_t // half
+        group = max(1, 8 // rows)
+        blocks = half // group
+
+        def gather_rows(which, index):
+            d, start = index // blocks, which * half + index % blocks * group
+            source = d * n_t + start
+            block = jnp.concatenate(
+                [normed_recv[source + k].astype(jnp.float32) for k in range(group)], axis=0
             )
-        ]
-        for load in loads:
-            load.start()
+            start = source * rows
+            if not isinstance(start, int):
+                start = pl.multiple_of(start, group * rows)
+            normed_all[pl.ds(start, group * rows), :] = block
+
+        fetch((gkv_hbm, gkv), (kv_up_hbm, kv_up), (gq_hbm, gq), (q_up_hbm, q_up))
 
         barrier = pltpu.get_barrier_semaphore()
 
@@ -195,6 +186,11 @@
         @pl.when(am_first)
         def _():
             pl.semaphore_wait(barrier, nears - 1)
+
+        @pl.when(am_last)
+        def _():
+            pl.semaphore_wait(barrier, devices - 1)
+            each(near, False, permit)
 
         for load in loads[:4]:
             load.wait()
@@ -216,10 +212,7 @@
 
         @pl.when(am_last)
         def _():
-            pl.semaphore_wait(barrier, devices - 1)
-            each(first, False, send_normed)
-            each(near, False, permit)
-            each(middle, False, send_normed)
+            each(near, False, send_normed)
 
         normed_recv[me] = normed_send[me_d]
         nt = (((1,), (1,)), ((), ()))
@@ -291,14 +284,15 @@
         wait_bytes(g_recv.at[pl.ds(0, n_t - 1)], send_sem.at[0])
         wait_bytes(all_grads.at[pl.ds(0, n_dp - 1)], send_sem.at[1])
         wait_bytes(normed_recv.at[pl.ds(0, devices - 1)], send_sem.at[2])
+        wait_bytes(g_recv.at[pl.ds(0, n_t - 1)], recv_sem.at[0])
 
     pl.run_scoped(
         talk,
         pltpu.SemaphoreType.DMA((8,)),
         pltpu.SemaphoreType.DMA((3,)),
+        pltpu.SemaphoreType.DMA((4,)),
         pltpu.SemaphoreType.REGULAR,
     )
-    wait_bytes(g_recv.at[pl.ds(0, n_t - 1)], recv_sem.at[0])
 
 
 def finish(
@@ -376,7 +370,6 @@
                 *(like(x) for x in operands[4:6]),
                 pltpu.VMEM((n_dp, rows, part), bf16),
                 like(passed[0]),
-                pltpu.SemaphoreType.DMA((4,)),
             ],
             compiler_params=pltpu.CompilerParams(
                 collective_id=0, has_side_effects=True, vmem_limit_bytes=LIMIT

time: 11.5 us -> 11.5 us (level)
  no operation moved by 1% of the time
where the time goes in v5:
time: 11.5 us; the launch traced here: 11.3 us
  Pallas kernels  10.7 us (93%)
  between operations  0.63 us (5%)
    pallas_call x1, Pallas kernels, body(): pl.pallas_call(functools.partial(exchange, n_dp, n_t), out_shape=passed,...  9.75 us
    pallas_call x1, Pallas kernels, body(): pl.pallas_call(finish, out_shape=results, in_specs=[vmem] * len(arrived),...  0.93 us

profile of v5, /device:TPU:0, one launch (start us, length us, event | category | flops | bytes accessed | tf_op | source)
XLA Modules:
  0.0 11.3 jit_solution(7042370174024002526)
XLA Ops:
  0.6 9.8 %shard_map.111 = (bf16[8,2,2048]{2,1,0:T(2,128)(2,1)S(1)}, bf16[4,16,896]{2,1,0:T(8,128)(2,1)S(1)}, f32[64,512]{1,0:T(8,128)S(1)}, f32[2,1536]{1,0:T(2,128)S(1)}...) custom-call(bf16[2,1536]{1,0:T(2,128)(2,1)} %lq_hbm.1, ...), custom_call_target="tpu_custom_call" | custom-call | tf_op jit(solution)/shard_map/pallas_call | solution.py:361
  10.4 0.9 %shard_map.112 = (f32[2,1536]{1,0:T(2,128)}, f32[2,512]{1,0:T(2,128)}, f32[384,384]{1,0:T(8,128)}, f32[128,512]{1,0:T(8,128)}) custom-call(bf16[8,2,2048]{2,1,0:T(2,128)(2,1)S(1)} %get-tuple-element.15.g, bf16[4,16,896]{2,1,0:T(8,128)(2,1)S(1)} %get-tuple-element.16.all_grads, f32[64,512]{1,0:T(8,128)S(1)} %get-tuple-element.17.normed_all, ...), custom_call_target="tpu_custom_call" | custom-call | tf_op jit(solution)/shard_map/pallas_call | solution.py:379

commit v6 on v5

--- a/solution.py
+++ b/solution.py
@@ -299,27 +299,29 @@
     g, all_grads, normed_all, unit_q, unit_kv, inverse_q, inverse_kv, gain_q, gain_kv, d_q, d_kv,
     out_q_hbm, out_kv_hbm, d_q_hbm, d_kv_hbm,
     out_q, out_kv,
-    store_sem,
 ):
-    stores = []
-
-    def store(source, target):
-        stores.append(pltpu.make_async_copy(source, target, store_sem.at[len(stores)]))
-        stores[-1].start()
-
-    store(d_q, d_q_hbm)
-    n_t = g.shape[0]
-    q_width = unit_q.shape[1]
-    store(d_kv, d_kv_hbm)
-    total = g[0].astype(jnp.float32)
-    for t in range(1, n_t):
-        total += g[t].astype(jnp.float32)
-    out_q[...] = backward_of_norm(total[:, :q_width], unit_q[...], inverse_q[...], gain_q[...])
-    out_kv[...] = backward_of_norm(total[:, q_width:], unit_kv[...], inverse_kv[...], gain_kv[...])
-    store(out_q, out_q_hbm)
-    store(out_kv, out_kv_hbm)
-    for copy in stores:
-        copy.wait()
+    def work(store_sem):
+        stores = []
+
+        def store(source, target):
+            stores.append(pltpu.make_async_copy(source, target, store_sem.at[len(stores)]))
+            stores[-1].start()
+
+        store(d_q, d_q_hbm)
+        n_t = g.shape[0]
+        q_width = unit_q.shape[1]
+        store(d_kv, d_kv_hbm)
+        total = g[0].astype(jnp.float32)
+        for t in range(1, n_t):
+            total += g[t].astype(jnp.float32)
+        out_q[...] = backward_of_norm(total[:, :q_width], unit_q[...], inverse_q[...], gain_q[...])
+        out_kv[...] = backward_of_norm(total[:, q_width:], unit_kv[...], inverse_kv[...], gain_kv[...])
+        store(out_q, out_q_hbm)
+        store(out_kv, out_kv_hbm)
+        for copy in stores:
+            copy.wait()
+
+    pl.run_scoped(work, pltpu.SemaphoreType.DMA((4,)))
 
 
 def solution(mesh):
@@ -383,7 +385,6 @@
             out_specs=(hbm,) * 4,
             scratch_shapes=[
                 *(like(x) for x in results[:2]),
-                pltpu.SemaphoreType.DMA((4,)),
             ],
             compiler_params=pltpu.CompilerParams(vmem_limit_bytes=LIMIT),
         )(*arrived)

time: 11.5 us -> 11.4 us (level)
  no operation moved by 1% of the time
where the time goes in v6:
time: 11.4 us; the launch traced here: 11.3 us
  Pallas kernels  10.6 us (93%)
  between operations  0.63 us (6%)
    pallas_call x1, Pallas kernels, body(): pl.pallas_call(functools.partial(exchange, n_dp, n_t), out_shape=passed,...  9.75 us
    pallas_call x1, Pallas kernels, body(): pl.pallas_call(finish, out_shape=results, in_specs=[vmem] * len(arrived),...  0.9 us

profile of v6, /device:TPU:0, one launch (start us, length us, event | category | flops | bytes accessed | tf_op | source)
XLA Modules:
  0.0 11.3 jit_solution(12936088942118505732)
XLA Ops:
  0.6 9.8 %shard_map.111 = (bf16[8,2,2048]{2,1,0:T(2,128)(2,1)S(1)}, bf16[4,16,896]{2,1,0:T(8,128)(2,1)S(1)}, f32[64,512]{1,0:T(8,128)S(1)}, f32[2,1536]{1,0:T(2,128)S(1)}...) custom-call(bf16[2,1536]{1,0:T(2,128)(2,1)} %lq_hbm.1, ...), custom_call_target="tpu_custom_call" | custom-call | tf_op jit(solution)/shard_map/pallas_call | solution.py:363
  10.4 0.9 %shard_map.112 = (f32[2,1536]{1,0:T(2,128)}, f32[2,512]{1,0:T(2,128)}, f32[384,384]{1,0:T(8,128)}, f32[128,512]{1,0:T(8,128)}) custom-call(bf16[8,2,2048]{2,1,0:T(2,128)(2,1)S(1)} %get-tuple-element.15.g, bf16[4,16,896]{2,1,0:T(8,128)(2,1)S(1)} %get-tuple-element.16.all_grads, f32[64,512]{1,0:T(8,128)S(1)} %get-tuple-element.17.normed_all, ...), custom_call_target="tpu_custom_call" | custom-call | tf_op jit(solution)/shard_map/pallas_call | solution.py:381

commit v7 on v6

--- a/solution.py
+++ b/solution.py
@@ -9,6 +9,7 @@
 
 EPS = 1e-06
 UNROLL = 64
+PARTS = 4
 LIMIT = 24 * 1024 * 1024
 
 
@@ -129,9 +130,9 @@
 
             repeat(count, step)
 
-        half = n_t // 2
+        half = n_t // PARTS
         my_half = me_t // half
-        group = max(1, 8 // rows)
+        group = min(max(1, 8 // rows), half)
         blocks = half // group
 
         def gather_rows(which, index):
@@ -266,7 +267,7 @@
             grads_to(remote)
 
         wait_bytes(all_grads.at[pl.ds(0, n_dp - 1)], recv_sem.at[1])
-        for which in range(2):
+        for which in range(PARTS):
             count = n_dp * half
 
             @pl.when(my_half == which)
@@ -290,7 +291,7 @@
         talk,
         pltpu.SemaphoreType.DMA((8,)),
         pltpu.SemaphoreType.DMA((3,)),
-        pltpu.SemaphoreType.DMA((4,)),
+        pltpu.SemaphoreType.DMA((2 + PARTS,)),
         pltpu.SemaphoreType.REGULAR,
     )
 

time: 11.4 us -> 11.4 us (level)
  no operation moved by 1% of the time
where the time goes in v7:
time: 11.4 us; the launch traced here: 11.3 us
  Pallas kernels  10.6 us (93%)
  between operations  0.63 us (6%)
    pallas_call x1, Pallas kernels, body(): pl.pallas_call(functools.partial(exchange, n_dp, n_t), out_shape=passed,...  9.74 us
    pallas_call x1, Pallas kernels, body(): pl.pallas_call(finish, out_shape=results, in_specs=[vmem] * len(arrived),...  0.9 us

profile of v7, /device:TPU:0, one launch (start us, length us, event | category | flops | bytes accessed | tf_op | source)
XLA Modules:
  0.0 11.3 jit_solution(16393634260425791800)
XLA Ops:
  0.6 9.7 %shard_map.111 = (bf16[8,2,2048]{2,1,0:T(2,128)(2,1)S(1)}, bf16[4,16,896]{2,1,0:T(8,128)(2,1)S(1)}, f32[64,512]{1,0:T(8,128)S(1)}, f32[2,1536]{1,0:T(2,128)S(1)}...) custom-call(bf16[2,1536]{1,0:T(2,128)(2,1)} %lq_hbm.1, ...), custom_call_target="tpu_custom_call" | custom-call | tf_op jit(solution)/shard_map/pallas_call | solution.py:364
  10.4 0.9 %shard_map.112 = (f32[2,1536]{1,0:T(2,128)}, f32[2,512]{1,0:T(2,128)}, f32[384,384]{1,0:T(8,128)}, f32[128,512]{1,0:T(8,128)}) custom-call(bf16[8,2,2048]{2,1,0:T(2,128)(2,1)S(1)} %get-tuple-element.15.g, bf16[4,16,896]{2,1,0:T(8,128)(2,1)S(1)} %get-tuple-element.16.all_grads, f32[64,512]{1,0:T(8,128)S(1)} %get-tuple-element.17.normed_all, ...), custom_call_target="tpu_custom_call" | custom-call | tf_op jit(solution)/shard_map/pallas_call | solution.py:382
